TPU v7x, 256 devices: a whole 4x4x8 slice. The times are simulated.
256 devices in a mesh: seq: 32 (over y, z), head: 8 (over x, core).
Axes of the slice: x: 4, y: 4, z: 8, core: 2. Of those that a mesh axis runs over, the one named last changes fastest.
Arguments:
- tokens: bfloat16 [32768, 2048], P(('seq', 'head')), may hold values from -6 to 6
- w_in_x: bfloat16 [2048, 4096], P(None, 'head'), may hold values from -0.125 to 0.125
- w_in_z: bfloat16 [2048, 4096], P(None, 'head'), may hold values from -0.125 to 0.125
- w_in_bc: bfloat16 [2048, 256], replicated, may hold values from -0.125 to 0.125
- w_dt: bfloat16 [2048, 64], P(None, 'head'), may hold values from -0.125 to 0.125
- conv_x: float32 [4, 4096], P(None, 'head'), may hold values from -3 to 3
- conv_bc: float32 [4, 256], replicated, may hold values from -3 to 3
- dt_bias: float32 [64], P('head'), may hold values from -1 to 1
- decay_rate: float32 [64], P('head'), may hold values from 1.5258789e-06 to 0.05, as said below
- skip: float32 [64], P('head'), may hold values from 0.5 to 1.5
- norm_gain: float32 [4096], P('head'), may hold values from 0.25 to 1.75
- w_out: bfloat16 [4096, 2048], P('head'), may hold values from -0.09375 to 0.09375
Outputs:
- mixed: bfloat16 [32768, 2048], P(('seq', 'head'))
Inputs may be any that keep to these rules, and one draw needn't show every extreme that they name: `decay_rate`: positive per-head decay rates.
All inputs are finite; a program needn't handle non-finite values.
Results may differ from a plain program's by a relative error of at most 0.013.
Values may be sent and summed in bfloat16 or wider, within the bound.
No kernel may reach another device: no remote copies, remote signals or barrier semaphores. Data moves between devices by JAX's collectives and lax.ppermute only.
A program may use at most 128 MiB of HBM per device.

v0:
```python
import jax
import jax.numpy as jnp
from jax import lax
from jax.sharding import Mesh
from jax.sharding import PartitionSpec as P

SPAN = 256
KERNEL = 4
E = 4096
SEQ = ("seq_0", "seq_1")
SEQ_HEAD = ("seq_0", "seq_1", "head")
highest = lax.Precision.HIGHEST


def passed_along(block, axis, distance):
    devices = range(lax.axis_size(axis))
    route = [(i - distance, i) for i in devices if i - distance in devices]
    return lax.ppermute(block, axis, route)


def neutral_like(shard, identity):
    return jax.tree.map(
        lambda part, zero: jnp.zeros_like(part) + jnp.asarray(zero, part.dtype), shard, identity
    )


def entering_2(shard, axes, combine, identity):
    before = start = neutral_like(shard, identity)
    running = shard
    for axis in reversed(axes):
        size, index = (lax.axis_size(axis), lax.axis_index(axis))
        pieces = jax.tree.map(lambda part: lax.all_gather(part, axis), running)
        inside, running = (start, start)
        for k in range(size):
            passed = k < index
            running = combine(running, jax.tree.map(lambda part: part[k], pieces))
            inside = jax.tree.map(lambda new, old: jnp.where(passed, new, old), running, inside)
        before = combine(inside, before)
    return before


def sent_to_all(shard, axis):
    size = lax.axis_size(axis)
    return lax.all_to_all(
        jnp.broadcast_to(shard[None], (size, *shard.shape)), axis, 0, 0, tiled=True
    )


def over_copies(shard, axis):
    everything = sent_to_all(shard, axis)
    return jnp.sum(everything, axis=0)


def span_update(state, x_span, step_span, decay_span, b_span, c_span, skip):
    cumul = jnp.cumsum(decay_span, axis=0)
    length = x_span.shape[0]
    lower = jnp.arange(length)[:, None] >= jnp.arange(length)[None, :]
    spread = cumul.T[:, :, None] - cumul.T[:, None, :]
    within = jnp.exp(jnp.where(lower[None], spread, -jnp.inf))
    scores = jnp.dot(c_span, b_span.T, precision=highest)
    scaled = x_span * step_span[:, :, None]
    output = jnp.einsum("hts,shp->thp", within * scores[None], scaled, precision=highest)
    output = (
        output
        + jnp.einsum("tn,hpn->thp", c_span, state, precision=highest) * jnp.exp(cumul)[:, :, None]
    )
    output = output + skip[None, :, None] * x_span
    remain = jnp.exp(cumul[-1][None, :] - cumul)
    fresh = jnp.einsum("shp,sn->hpn", scaled * remain[:, :, None], b_span, precision=highest)
    return (jnp.exp(cumul[-1])[:, None, None] * state + fresh, output, cumul)


def causal_conv(values, before, kernel):
    padded = jnp.concatenate([before, values], axis=0)
    length = values.shape[0]
    result = kernel[0] * padded[0:length]
    for offset in range(1, kernel.shape[0]):
        result = result + kernel[offset] * padded[offset : offset + length]
    return jax.nn.silu(result)


def per_device(
    tokens,
    w_in_x,
    w_in_z,
    w_in_bc,
    w_dt,
    conv_x,
    conv_bc,
    dt_bias,
    decay_rate,
    skip,
    norm_gain,
    w_out,
):
    inner_cols = w_in_x.shape[1]
    head_count = dt_bias.shape[0]
    head_width = inner_cols // head_count
    state_size = w_in_bc.shape[1] // 2
    block_rows = lax.all_gather(tokens, "head", axis=0, tiled=True)
    joined = jnp.concatenate(
        [
            jnp.dot(block_rows, w_in_x, preferred_element_type=jnp.float32),
            jnp.dot(block_rows, w_in_z, preferred_element_type=jnp.float32),
            jnp.dot(block_rows, w_in_bc, preferred_element_type=jnp.float32),
            jnp.dot(block_rows, w_dt, preferred_element_type=jnp.float32),
        ],
        axis=1,
    )
    x_proj = joined[:, :inner_cols]
    gate_proj = joined[:, inner_cols : 2 * inner_cols]
    bc_proj = joined[:, 2 * inner_cols : 2 * inner_cols + 2 * state_size]
    step_raw = joined[:, 2 * inner_cols + 2 * state_size :]
    margin = KERNEL - 1
    x_before, bc_before = passed_along((x_proj[-margin:], bc_proj[-margin:]), SEQ, 1)
    x_conv = causal_conv(x_proj, x_before, conv_x)
    bc_conv = causal_conv(bc_proj, bc_before, conv_bc)
    step_size = jax.nn.softplus(step_raw + dt_bias)
    log_decay = -step_size * decay_rate
    seg_rows = x_proj.shape[0]
    spans = seg_rows // SPAN

    def advance(carry, inputs):
        state, offset = carry
        x_span, step_span, decay_span, bc_span = inputs
        state, output, cumul = span_update(
            state,
            x_span,
            step_span,
            decay_span,
            bc_span[:, :state_size],
            bc_span[:, state_size:],
            skip,
        )
        return ((state, offset + cumul[-1]), (output, cumul + offset))

    empty_state = jnp.zeros((head_count, head_width, state_size), jnp.float32)
    empty_decay = jnp.zeros((head_count,), jnp.float32)
    (final_state, totals), (outputs, cumuls) = lax.scan(
        advance,
        (empty_state, empty_decay),
        (
            x_conv.reshape(spans, SPAN, head_count, head_width),
            step_size.reshape(spans, SPAN, head_count),
            log_decay.reshape(spans, SPAN, head_count),
            bc_conv.reshape(spans, SPAN, 2 * state_size),
        ),
    )
    local_out = outputs.reshape(seg_rows, head_count, head_width)
    segment_cumul = cumuls.reshape(seg_rows, head_count)

    def combine(earlier, later):
        return (earlier[0] + later[0], jnp.exp(later[0])[:, None, None] * earlier[1] + later[1])

    entering = entering_2((totals, final_state), SEQ, combine, (empty_decay, empty_state))[1]
    c_matrix = bc_conv[:, state_size:]
    carried = (
        jnp.einsum("tn,hpn->thp", c_matrix, entering, precision=highest)
        * jnp.exp(segment_cumul)[:, :, None]
    )
    ssd_out = (local_out + carried).reshape(seg_rows, inner_cols)
    gated = ssd_out * jax.nn.silu(gate_proj)
    squares = over_copies(jnp.sum(gated * gated, axis=1), "head")
    normed = (gated * lax.rsqrt(squares / E + 1e-05)[:, None] * norm_gain).astype(jnp.bfloat16)
    result = lax.psum_scatter(
        jnp.dot(normed, w_out, preferred_element_type=jnp.float32).astype(jnp.bfloat16),
        "head",
        scatter_dimension=0,
        tiled=True,
    )
    return result


def solution(mesh):
    torus = Mesh(mesh.devices.reshape(4, 8, mesh.shape["head"]), ("seq_0", "seq_1", "head"))
    placed = (
        P(SEQ_HEAD, None),
        P(None, "head"),
        P(None, "head"),
        P(),
        P(None, "head"),
        P(None, "head"),
        P(),
        P("head"),
        P("head"),
        P("head"),
        P("head"),
        P("head", None),
    )
    return jax.shard_map(
        per_device, mesh=torus, in_specs=placed, out_specs=P(SEQ_HEAD, None), check_vma=False
    )
```

profile of v0, /device:TPU:8, one launch (start us, length us, event | category | flops | bytes accessed | tf_op | source)
XLA Modules:
  0.0 303.0 jit_solution(5351362348094303624)
XLA Ops:
  9.0 37.6 %all-gather.7.cloned.1.call-done = bf16[1024,2048]{1,0:T(8,128)(2,1)} async-done(((bf16[128,2048]{1,0:T(8,128)(2,1)}), bf16[1024,2048]{1,0:T(8,128)(2,1)}) %all-gather.7.cloned.1.call-update) | async-done | bytes 4194320 | tf_op jit(solution)/shard_map/all_gather | solution.py:100
  46.7 3.9 %fusion.150 = f32[1024,256]{1,0:T(8,128)S(1)} fusion(bf16[1024,2048]{1,0:T(8,128)(2,1)} %all-gather.7.cloned.1.call-done, bf16[2048,256]{1,0:T(8,128)(2,1)} %param.17), kind=kOutput, calls=%fused_computation.216 | convolution fusion | flops 1073741824 | bytes 6291456 | tf_op jit(solution)/shard_map/dot_general | solution.py:105
  50.6 3.6 %collective-permute-start.1 = (f32[3,256]{1,0:T(4,128)S(1)}, f32[3,256]{1,0:T(4,128)S(1)}, u32[]{:S(2)}, u32[]{:S(2)}) collective-permute-start(f32[3,256]{1,0:T(4,128)S(1)} %slice.215), channel_id=1, source_target_pairs={{0,8},{8,16},{16,24},{24,32},{32,40},{40,48},{48,56},{56,64},{64,7... | collective-permute-start | bytes 9224 | tf_op jit(solution)/shard_map/ppermute | solution.py:18
  56.6 3.5 %collective-permute-start = (f32[3,512]{1,0:T(4,128)S(1)}, f32[3,512]{1,0:T(4,128)S(1)}, u32[]{:S(2)}, u32[]{:S(2)}) collective-permute-start(f32[3,512]{1,0:T(4,128)S(1)} %slice.210), channel_id=1, source_target_pairs={{0,8},{8,16},{16,24},{24,32},{32,40},{40,48},{48,56},{56,64},{64,7... | collective-permute-start | bytes 18440 | tf_op jit(solution)/shard_map/ppermute | solution.py:18
  66.5 4.4 %reshape.345 = f32[4,256,8,64]{3,2,1,0:T(8,128)} reshape(f32[1024,512]{1,0:T(8,128)} %divide_multiply_fusion) | data formatting | bytes 4194304 | tf_op jit(solution)/shard_map/reshape | solution.py:143
  70.9 3.8 %copy.48 = f32[4,256,8,64]{1,3,2,0:T(8,128)} copy(f32[4,256,8,64]{3,2,1,0:T(8,128)} %reshape.345) | data formatting | bytes 4194304
  74.7 81.7 %while.17 = (s32[]{:T(128)}, f32[8,64,128]{2,1,0:T(8,128)S(1)}, f32[8]{0:T(128)S(1)}, f32[4,256,8,64]{1,0,3,2:T(4,128)}, f32[4,256,8]{1,2,0:T(8,128)S(1)}, /*ind...) while((s32[]{:T(128)}, f32[8,64,128]{2,1,0:T(8,128)S(1)}, ...), condition=%wide.region_3.4_spmd.clone, body=%wide.region_0.3_spmd.clone.sunk | while | flops 909056064 | bytes 16289238 | solution.py:139
  77.5 3.5 %fusion.182 = f32[256,8,64]{0,2,1:T(8,128)S(1)} fusion(f32[256,256]{1,0:T(8,128)S(1)} %fusion.181, f32[8,256]{1,0:T(8,128)S(1)} %add_bitcast_fusion.4, pred[256,256]{1,0:T(8,128)(4,1)S(1)} %iota_compare_fusion.2, f32[4,256,8,64]{1,3,2,0:T(8,128)} %get-tuple-element.315, s32[]{:T(128)S(6)} %copy.71, f32[256,8]{0,1:T(8,128)S(1)} %dynamic-slice_bitcast_fusion.7), kind=kOutput, calls=%fused_computation.5.clone.1 | convolution fusion | flops 404357120 | bytes 1400836 | tf_op jit(solution)/shard_map/while/body/eval_jaxpr/hts,shp->thp/dot_general | solution.py:62
  82.9 12.3 %dynamic_update_slice.14 = f32[4,256,8,64]{1,0,3,2:T(4,128)} dynamic-update-slice(f32[4,256,8,64]{1,0,3,2:T(4,128)} %get-tuple-element.299, f32[1,256,8,64]{1,0,3,2:T(1,128)S(1)} %copy.63, s32[]{:T(128)S(6)} %copy.71, s32[]{:T(128)} %constant.25.clone.1..sunk, s32[]{:T(128)} %constant.25.clone.1..sunk, s32[]{:T(128)} %constant.25.clone.1..sunk) | dynamic-update-slice | bytes 1048580 | tf_op jit(solution)/shard_map/while/body/jit(dynamic_update_index_in_dim)/dynamic_update_slice | solution.py:139
  97.9 3.5 %fusion.182 = f32[256,8,64]{0,2,1:T(8,128)S(1)} fusion(f32[256,256]{1,0:T(8,128)S(1)} %fusion.181, f32[8,256]{1,0:T(8,128)S(1)} %add_bitcast_fusion.4, pred[256,256]{1,0:T(8,128)(4,1)S(1)} %iota_compare_fusion.2, f32[4,256,8,64]{1,3,2,0:T(8,128)} %get-tuple-element.315, s32[]{:T(128)S(6)} %copy.71, f32[256,8]{0,1:T(8,128)S(1)} %dynamic-slice_bitcast_fusion.7), kind=kOutput, calls=%fused_computation.5.clone.1 | convolution fusion | flops 404357120 | bytes 1400836 | tf_op jit(solution)/shard_map/while/body/eval_jaxpr/hts,shp->thp/dot_general | solution.py:62
  103.3 12.3 %dynamic_update_slice.14 = f32[4,256,8,64]{1,0,3,2:T(4,128)} dynamic-update-slice(f32[4,256,8,64]{1,0,3,2:T(4,128)} %get-tuple-element.299, f32[1,256,8,64]{1,0,3,2:T(1,128)S(1)} %copy.63, s32[]{:T(128)S(6)} %copy.71, s32[]{:T(128)} %constant.25.clone.1..sunk, s32[]{:T(128)} %constant.25.clone.1..sunk, s32[]{:T(128)} %constant.25.clone.1..sunk) | dynamic-update-slice | bytes 1048580 | tf_op jit(solution)/shard_map/while/body/jit(dynamic_update_index_in_dim)/dynamic_update_slice | solution.py:139
  118.4 3.5 %fusion.182 = f32[256,8,64]{0,2,1:T(8,128)S(1)} fusion(f32[256,256]{1,0:T(8,128)S(1)} %fusion.181, f32[8,256]{1,0:T(8,128)S(1)} %add_bitcast_fusion.4, pred[256,256]{1,0:T(8,128)(4,1)S(1)} %iota_compare_fusion.2, f32[4,256,8,64]{1,3,2,0:T(8,128)} %get-tuple-element.315, s32[]{:T(128)S(6)} %copy.71, f32[256,8]{0,1:T(8,128)S(1)} %dynamic-slice_bitcast_fusion.7), kind=kOutput, calls=%fused_computation.5.clone.1 | convolution fusion | flops 404357120 | bytes 1400836 | tf_op jit(solution)/shard_map/while/body/eval_jaxpr/hts,shp->thp/dot_general | solution.py:62
  123.7 12.3 %dynamic_update_slice.14 = f32[4,256,8,64]{1,0,3,2:T(4,128)} dynamic-update-slice(f32[4,256,8,64]{1,0,3,2:T(4,128)} %get-tuple-element.299, f32[1,256,8,64]{1,0,3,2:T(1,128)S(1)} %copy.63, s32[]{:T(128)S(6)} %copy.71, s32[]{:T(128)} %constant.25.clone.1..sunk, s32[]{:T(128)} %constant.25.clone.1..sunk, s32[]{:T(128)} %constant.25.clone.1..sunk) | dynamic-update-slice | bytes 1048580 | tf_op jit(solution)/shard_map/while/body/jit(dynamic_update_index_in_dim)/dynamic_update_slice | solution.py:139
  138.8 3.5 %fusion.182 = f32[256,8,64]{0,2,1:T(8,128)S(1)} fusion(f32[256,256]{1,0:T(8,128)S(1)} %fusion.181, f32[8,256]{1,0:T(8,128)S(1)} %add_bitcast_fusion.4, pred[256,256]{1,0:T(8,128)(4,1)S(1)} %iota_compare_fusion.2, f32[4,256,8,64]{1,3,2,0:T(8,128)} %get-tuple-element.315, s32[]{:T(128)S(6)} %copy.71, f32[256,8]{0,1:T(8,128)S(1)} %dynamic-slice_bitcast_fusion.7), kind=kOutput, calls=%fused_computation.5.clone.1 | convolution fusion | flops 404357120 | bytes 1400836 | tf_op jit(solution)/shard_map/while/body/eval_jaxpr/hts,shp->thp/dot_general | solution.py:62
  144.1 12.3 %dynamic_update_slice.14 = f32[4,256,8,64]{1,0,3,2:T(4,128)} dynamic-update-slice(f32[4,256,8,64]{1,0,3,2:T(4,128)} %get-tuple-element.299, f32[1,256,8,64]{1,0,3,2:T(1,128)S(1)} %copy.63, s32[]{:T(128)S(6)} %copy.71, s32[]{:T(128)} %constant.25.clone.1..sunk, s32[]{:T(128)} %constant.25.clone.1..sunk, s32[]{:T(128)} %constant.25.clone.1..sunk) | dynamic-update-slice | bytes 1048580 | tf_op jit(solution)/shard_map/while/body/jit(dynamic_update_index_in_dim)/dynamic_update_slice | solution.py:139
  158.8 15.8 %all-reduce = f32[64]{0:T(128)S(1)} all-reduce(f32[64]{0:T(128)S(1)} %dynamic-update-slice), channel_id=2, replica_groups=mesh['seq_0'=4,'seq_1'=8,'head'=8] {'seq_1'}, use_global_device_ids=true, to_apply=%add | all-reduce | flops 64 | bytes 512
  174.7 21.7 %all-gather.11.cloned.1.call-done = f32[64,64,128]{2,1,0:T(8,128)} async-done(((f32[8,64,128]{2,1,0:T(8,128)}), f32[64,64,128]{2,1,0:T(8,128)}) %all-gather.11.cloned.1.call-update) | async-done | bytes 2097168 | tf_op jit(solution)/shard_map/all_gather | solution.py:32
  198.9 7.8 %all-gather.2 = f32[4,1,8]{2,1,0:T(1,128)S(1)} all-gather(f32[1,1,8]{2,1,0:T(1,128)S(1)} %get-tuple-element.197), channel_id=1, replica_groups=mesh['seq_0'=4,'seq_1'=8,'head'=8] {'seq_0'}, dimensions={0}, use_global_device_ids=true | all-gather | bytes 160 | tf_op jit(solution)/shard_map/all_gather | solution.py:32
  210.0 13.0 %all-gather.9.cloned.1.call-done = f32[4,8,64,128]{3,2,1,0:T(8,128)} async-done(((f32[1,8,64,128]{3,2,1,0:T(8,128)}), f32[4,8,64,128]{3,2,1,0:T(8,128)}) %all-gather.9.cloned.1.call-update) | async-done | bytes 1048592 | tf_op jit(solution)/shard_map/all_gather | solution.py:32
  223.1 6.3 %multiply_add_fusion = f32[1024,8,64]{0,2,1:T(8,128)} fusion(f32[1024,8,64]{0,2,1:T(8,128)} %reshape.235, f32[1024,8]{0,1:T(8,128)S(1)} %bitcast.186, f32[1024,256]{1,0:T(8,128)} %divide_multiply_fusion.1, f32[4,8,64,128]{3,2,1,0:T(8,128)} %all-gather.9.cloned.1.call-done, f32[64,64,128]{2,1,0:T(8,128)} %all-gather.11.cloned.1.call-done, ...), kind=kOutput, calls=%fused_computation.64 | convolution fusion | flops 808714240 | bytes 7897516 | tf_op jit(solution)/shard_map/tn,hpn->thp/dot_general | solution.py:158
  232.2 7.4 %multiply_reduce_fusion = (f32[1024]{0:T(1024)S(1)}, f32[1024,512]{1,0:T(8,128)}) fusion(f32[1024,512]{1,0:T(8,128)} %copy.52, bf16[1024,2048]{1,0:T(8,128)(2,1)} %all-gather.7.cloned.1.call-done, bf16[2048,512]{1,0:T(8,128)(2,1)} %param.16), kind=kOutput, calls=%fused_computation.62 | convolution fusion | flops 2151152640 | bytes 10489856 | tf_op jit(solution)/shard_map/dot_general | solution.py:104
  239.6 9.5 %all_to_all.6 = f32[8,1,1024]{2,1,0:T(1,128)S(1)} all-to-all(f32[8,1,1024]{2,1,0:T(1,128)S(1)} %broadcast_in_dim.43), channel_id=1, replica_groups=mesh['seq_0'=4,'seq_1'=8,'head'=8] {'head'}, dimensions={0} | all-to-all | bytes 65536 | tf_op jit(solution)/shard_map/all_to_all | solution.py:44
  249.2 6.9 %convolution_convert_fusion = bf16[1024,2048]{1,0:T(8,128)(2,1)} fusion(bf16[512,2048]{1,0:T(8,128)(2,1)S(1)} %copy-done, f32[512]{0:T(512)S(1)} %copy-done.9, f32[1024]{0:T(1024)S(1)} %add_rsqrt_fusion, f32[1024,512]{1,0:T(8,128)} %copy.52, f32[1024,512]{1,0:T(8,128)} %get-tuple-element.209), kind=kOutput, calls=%fused_computation.49 | convolution fusion | flops 2153775104 | bytes 10491904 | tf_op jit(solution)/shard_map/dot_general | solution.py:166
  256.1 40.4 %reduce-scatter.2.cloned.1.call-done = bf16[128,2048]{1,0:T(8,128)(2,1)} async-done(((bf16[1024,2048]{1,0:T(8,128)(2,1)}), bf16[128,2048]{1,0:T(8,128)(2,1)}) %reduce-scatter.2.cloned.1.call-update) | async-done | bytes 524304 | tf_op jit(solution)/shard_map/reduce_scatter | solution.py:165
  (135 shorter events, 40.1 us)
Async XLA Ops:
  6.5 242.6 %copy-start = (bf16[512,2048]{1,0:T(8,128)(2,1)S(1)}, bf16[512,2048]{1,0:T(8,128)(2,1)}, u32[]{:S(2)}) copy-start(bf16[512,2048]{1,0:T(8,128)(2,1)} %param.25) | copy-start | bytes 6291460
  6.5 40.1 %all-gather.7.cloned.1.call-start = ((), (), s32[]{:S(2)}) async-start(), calls=%async_computation.2 | async-start | bytes 4718592 | tf_op jit(solution)/shard_map/all_gather | solution.py:100
  7.3 189.1 %all-gather.11.cloned.1.call-start = ((), (), s32[]{:S(2)}) async-start(), calls=%async_computation.5 | async-start | bytes 2359296 | tf_op jit(solution)/shard_map/all_gather | solution.py:32
  46.7 7.5 %copy-start.3 = (bf16[1024,2048]{1,0:T(8,128)(2,1)S(1)}, bf16[1024,2048]{1,0:T(8,128)(2,1)}, u32[]{:S(2)}) copy-start(bf16[1024,2048]{1,0:T(8,128)(2,1)} %all-gather.7.cloned.1.call-done) | copy-start | bytes 12582916
  46.7 7.6 %copy-start.8 = (bf16[2048,512]{1,0:T(8,128)(2,1)S(1)}, bf16[2048,512]{1,0:T(8,128)(2,1)}, u32[]{:S(2)}) copy-start(bf16[2048,512]{1,0:T(8,128)(2,1)} %param.15) | copy-start | bytes 6291460
  50.6 9.5 %copy-start.4 = (bf16[2048,8]{0,1:T(8,128)(2,1)S(1)}, bf16[2048,8]{0,1:T(8,128)(2,1)}, u32[]{:S(2)}) copy-start(bf16[2048,8]{0,1:T(8,128)(2,1)} %param.18) | copy-start | bytes 98308
  50.6 9.5 %copy-start.6 = (f32[8]{0:T(128)S(1)}, f32[8]{0:T(128)}, u32[]{:S(2)}) copy-start(f32[8]{0:T(128)} %param.22) | copy-start | bytes 100
  50.6 9.5 %copy-start.7 = (f32[8]{0:T(128)S(1)}, f32[8]{0:T(128)}, u32[]{:S(2)}) copy-start(f32[8]{0:T(128)} %param.21) | copy-start | bytes 100
  50.6 10.7 %collective-permute-start.1 = (f32[3,256]{1,0:T(4,128)S(1)}, f32[3,256]{1,0:T(4,128)S(1)}, u32[]{:S(2)}, u32[]{:S(2)}) collective-permute-start(f32[3,256]{1,0:T(4,128)S(1)} %slice.215), channel_id=1, source_target_pairs={{0,8},{8,16},{16,24},{24,32},{32,40},{40,48},{48,56},{56,64},{64,7... | collective-permute-start | bytes 9224 | tf_op jit(solution)/shard_map/ppermute | solution.py:18
  56.6 7.7 %collective-permute-start = (f32[3,512]{1,0:T(4,128)S(1)}, f32[3,512]{1,0:T(4,128)S(1)}, u32[]{:S(2)}, u32[]{:S(2)}) collective-permute-start(f32[3,512]{1,0:T(4,128)S(1)} %slice.210), channel_id=1, source_target_pairs={{0,8},{8,16},{16,24},{24,32},{32,40},{40,48},{48,56},{56,64},{64,7... | collective-permute-start | bytes 18440 | tf_op jit(solution)/shard_map/ppermute | solution.py:18
  70.9 3.8 %copy-start.5 = (f32[8]{0:T(128)S(1)}, f32[8]{0:T(128)}, u32[]{:S(2)}) copy-start(f32[8]{0:T(128)} %param.23) | copy-start | bytes 100
  74.7 82.5 %copy-start.10 = (u32[256]{0:T(256)S(1)}, u32[256]{0:T(256)}, u32[]{:S(2)}) copy-start(u32[256]{0:T(256)} %constant.70) | copy-start | bytes 3076
  76.0 5.0 %copy-start.2 = (f32[4,256,8,64]{1,3,2,0:T(8,128)S(1)}, f32[4,256,8,64]{1,3,2,0:T(8,128)}, u32[]{:S(2)}) copy-start(f32[4,256,8,64]{1,3,2,0:T(8,128)} %get-tuple-element.315) | copy-start | bytes 6291460 | tf_op jit(solution)/shard_map/while
  96.4 5.0 %copy-start.2 = (f32[4,256,8,64]{1,3,2,0:T(8,128)S(1)}, f32[4,256,8,64]{1,3,2,0:T(8,128)}, u32[]{:S(2)}) copy-start(f32[4,256,8,64]{1,3,2,0:T(8,128)} %get-tuple-element.315) | copy-start | bytes 6291460 | tf_op jit(solution)/shard_map/while
  116.8 5.0 %copy-start.2 = (f32[4,256,8,64]{1,3,2,0:T(8,128)S(1)}, f32[4,256,8,64]{1,3,2,0:T(8,128)}, u32[]{:S(2)}) copy-start(f32[4,256,8,64]{1,3,2,0:T(8,128)} %get-tuple-element.315) | copy-start | bytes 6291460 | tf_op jit(solution)/shard_map/while
  137.3 5.0 %copy-start.2 = (f32[4,256,8,64]{1,3,2,0:T(8,128)S(1)}, f32[4,256,8,64]{1,3,2,0:T(8,128)}, u32[]{:S(2)}) copy-start(f32[4,256,8,64]{1,3,2,0:T(8,128)} %get-tuple-element.315) | copy-start | bytes 6291460 | tf_op jit(solution)/shard_map/while
  156.4 0.7 copy-start.1
  157.1 65.9 %all-gather.9.cloned.1.call-start = ((), (), s32[]{:S(2)}) async-start(), calls=%async_computation.3 | async-start | bytes 1310720 | tf_op jit(solution)/shard_map/all_gather | solution.py:32
  198.8 97.6 %reduce-scatter.2.cloned.1.call-start = ((), (), s32[]{:S(2)}) async-start(), calls=%async_computation.4 | async-start | bytes 4718592 | tf_op jit(solution)/shard_map/reduce_scatter | solution.py:165
  232.2 17.0 %copy-start.9 = (f32[512]{0:T(512)S(1)}, f32[512]{0:T(512)}, u32[]{:S(2)}) copy-start(f32[512]{0:T(512)} %param.24) | copy-start | bytes 6148
Sparse Core Ops, SparseCore 0:
  9.2 37.4 all-gather.6
  157.3 39.0 all-gather.10
  199.0 24.0 all-gather.8
  256.2 40.2 reduce-scatter.1
where the time goes:
time: 305 us; the launch traced here: 303 us
  waiting for transfers between devices  115 us (38%)
  local copies, waits for them, and re-layouts  75.1 us (25%)
  matrix products  48.5 us (16%)
  blocking collectives  33.1 us (11%)
  between operations  14 us (5%)
  other arithmetic  10.2 us (3%)
  starting transfers between devices  7.17 us (2%)
    dynamic_update_slice x8, local copies, waits for them, and re-layouts, per_device(): lax.scan(advance, (empty_state, empty_decay), (x_conv.reshape(spans, SPAN...  51.4 us
    reduce_scatter x1, waiting for transfers between devices, per_device(): lax.psum_scatter(jnp.dot(normed, w_out, preferred_element_type=jnp.float3...  40.4 us
    all_gather x1, waiting for transfers between devices, per_device(): block_rows = lax.all_gather(tokens, 'head', axis=0, tiled=True)  37.6 us
    all_gather x2, waiting for transfers between devices, entering_2(): pieces = jax.tree.map(lambda part: lax.all_gather(part, axis), running)  34.7 us
    unnamed x1, blocking collectives  15.8 us
    dot_general x4, matrix products, span_update(): jnp.einsum('hts,shp->thp', within * scores[None], scaled, precision=highest)  13.9 us
    all_to_all x1, blocking collectives, sent_to_all(): lax.all_to_all(jnp.broadcast_to(shard[None], (size, *shard.shape)), axis,...  9.5 us
    all_gather x1, blocking collectives, entering_2(): pieces = jax.tree.map(lambda part: lax.all_gather(part, axis), running)  7.78 us
  transfers between devices with their start and end apart: 6, of which 5 were waited for; matrix products, arithmetic and copies ran while one was open for 4% of the time, Pallas kernels for 0%

commit v1 on v0

--- a/solution.py
+++ b/solution.py
@@ -97,7 +97,9 @@
     head_count = dt_bias.shape[0]
     head_width = inner_cols // head_count
     state_size = w_in_bc.shape[1] // 2
-    block_rows = lax.all_gather(tokens, "head", axis=0, tiled=True)
+    block_rows = jnp.concatenate(
+        lax.all_to_all(jnp.stack([tokens] * lax.axis_size("head")), "head", 0, 0), axis=0
+    )
     joined = jnp.concatenate(
         [
             jnp.dot(block_rows, w_in_x, preferred_element_type=jnp.float32),

time: 305 us -> 336 us (1.10)
  matrix products: 48.5 us -> 61 us
  waiting for transfers between devices: 115 us -> 124 us
  starting transfers between devices: 7.17 us -> 12.8 us
    all_to_all x0 -> x1, waiting for transfers between devices: none -> 49.5 us  [per_device(): lax.all_to_all(jnp.stack([tokens] * lax.axis_size('head')), 'head', 0, 0)]
    all_gather x1 -> x0, waiting for transfers between devices: 37.6 us -> none  [per_device(): block_rows = lax.all_gather(tokens, 'head', axis=0, tiled=True)]
    all_to_all x0 -> x1, starting transfers between devices: none -> 4.69 us  [per_device(): lax.all_to_all(jnp.stack([tokens] * lax.axis_size('head')), 'head', 0, 0)]
    dot_general x4, matrix products: 2.36 us -> 6.56 us  [span_update(): jnp.einsum('tn,hpn->thp', c_span, state, precision=highest)]
    dot_general x4, matrix products: 2.72 us -> 6.88 us  [span_update(): jnp.einsum('shp,sn->hpn', scaled * remain[:, :, None], b_span, precision=...]
    another operation x4 -> x5, local copies, waits for them, and re-layouts: 0.02 us -> 3.7 us  [the longest x1 3.68 us: per_device(): jnp.stack([tokens] * lax.axis_size('head'))]
  transfers between devices with their start and end apart: 6 -> 6, of which waited for: 5 -> 4; matrix products, arithmetic and copies ran while one was open for 4% -> 4% of each run, Pallas kernels for 0% -> 0%
where the time goes in v1:
time: 336 us; the launch traced here: 333 us
  waiting for transfers between devices  124 us (37%)
  local copies, waits for them, and re-layouts  76.6 us (23%)
  matrix products  61 us (18%)
  blocking collectives  34.4 us (10%)
  between operations  14.1 us (4%)
  starting transfers between devices  12.8 us (4%)
  other arithmetic  10.2 us (3%)
    dynamic_update_slice x8, local copies, waits for them, and re-layouts, per_device(): lax.scan(advance, (empty_state, empty_decay), (x_conv.reshape(spans, SPAN...  51.4 us
    all_to_all x1, waiting for transfers between devices, per_device(): lax.all_to_all(jnp.stack([tokens] * lax.axis_size('head')), 'head', 0, 0)  49.5 us
    reduce_scatter x1, waiting for transfers between devices, per_device(): lax.psum_scatter(jnp.dot(normed, w_out, preferred_element_type=jnp.float3...  40.4 us
    all_gather x2, waiting for transfers between devices, entering_2(): pieces = jax.tree.map(lambda part: lax.all_gather(part, axis), running)  34.1 us
    unnamed x1, blocking collectives  17.1 us
    dot_general x4, matrix products, span_update(): jnp.einsum('hts,shp->thp', within * scores[None], scaled, precision=highest)  13.9 us
    all_to_all x1, blocking collectives, sent_to_all(): lax.all_to_all(jnp.broadcast_to(shard[None], (size, *shard.shape)), axis,...  9.5 us
    all_gather x1, blocking collectives, entering_2(): pieces = jax.tree.map(lambda part: lax.all_gather(part, axis), running)  7.85 us
  transfers between devices with their start and end apart: 6, of which 4 were waited for; matrix products, arithmetic and copies ran while one was open for 4% of the time, Pallas kernels for 0%

profile of v1, /device:TPU:8, one launch (start us, length us, event | category | flops | bytes accessed | tf_op | source)
XLA Modules:
  0.0 333.5 jit_solution(8444597655974495141)
XLA Ops:
  6.5 3.7 %stack.2 = bf16[8,128,2048]{2,1,0:T(8,128)(2,1)} broadcast(bf16[128,2048]{1,0:T(8,128)(2,1)} %param.14), dimensions={1,2} | broadcast | bytes 4718592 | tf_op jit(solution)/shard_map/stack | solution.py:101
  10.2 4.7 %all-to-all-start = ((bf16[8,128,2048]{2,1,0:T(8,128)(2,1)}), bf16[8,128,2048]{2,1,0:T(8,128)(2,1)}, u32[]{:S(2)}, u32[]{:S(2)}) async-start(bf16[8,128,2048]{2,1,0:T(8,128)(2,1)} %stack.2), calls=%async_computation | async-start | bytes 8388608 | tf_op jit(solution)/shard_map/all_to_all | solution.py:101
  15.1 49.5 %all-to-all-done = bf16[8,128,2048]{2,1,0:T(8,128)(2,1)} async-done(((bf16[8,128,2048]{2,1,0:T(8,128)(2,1)}), bf16[8,128,2048]{2,1,0:T(8,128)(2,1)}, u32[]{:S(2)}, u32[]{:S(2)}) %all-to-all-start) | async-done | bytes 4194336 | tf_op jit(solution)/shard_map/all_to_all | solution.py:101
  64.6 3.9 %fusion.150 = f32[1024,256]{1,0:T(8,128)S(1)} fusion(bf16[1024,2048]{1,0:T(8,128)(2,1)} %bitcast, bf16[2048,256]{1,0:T(8,128)(2,1)} %param.17), kind=kOutput, calls=%fused_computation.216 | convolution fusion | flops 1073741824 | bytes 6291456 | tf_op jit(solution)/shard_map/dot_general | solution.py:107
  68.5 4.0 %collective-permute-start.1 = (f32[3,256]{1,0:T(4,128)S(1)}, f32[3,256]{1,0:T(4,128)S(1)}, u32[]{:S(2)}, u32[]{:S(2)}) collective-permute-start(f32[3,256]{1,0:T(4,128)S(1)} %slice.215), channel_id=1, source_target_pairs={{0,8},{8,16},{16,24},{24,32},{32,40},{40,48},{48,56},{56,64},{64,7... | collective-permute-start | bytes 9224 | tf_op jit(solution)/shard_map/ppermute | solution.py:18
  72.5 4.5 %fusion.149 = f32[1024,512]{1,0:T(8,128)S(1)} fusion(bf16[1024,2048]{1,0:T(8,128)(2,1)} %bitcast, bf16[2048,512]{1,0:T(8,128)(2,1)S(1)} %copy-done.9), kind=kOutput, calls=%fused_computation.215 | convolution fusion | flops 2147483648 | bytes 8388608 | tf_op jit(solution)/shard_map/dot_general | solution.py:105
  77.0 3.8 %collective-permute-start = (f32[3,512]{1,0:T(4,128)S(1)}, f32[3,512]{1,0:T(4,128)S(1)}, u32[]{:S(2)}, u32[]{:S(2)}) collective-permute-start(f32[3,512]{1,0:T(4,128)S(1)} %slice.210), channel_id=1, source_target_pairs={{0,8},{8,16},{16,24},{24,32},{32,40},{40,48},{48,56},{56,64},{64,7... | collective-permute-start | bytes 18440 | tf_op jit(solution)/shard_map/ppermute | solution.py:18
  88.2 4.4 %reshape.351 = f32[4,256,8,64]{3,2,1,0:T(8,128)} reshape(f32[1024,512]{1,0:T(8,128)} %divide_multiply_fusion) | data formatting | bytes 4194304 | tf_op jit(solution)/shard_map/reshape | solution.py:145
  92.7 3.8 %copy.48 = f32[4,256,8,64]{1,3,2,0:T(8,128)} copy(f32[4,256,8,64]{3,2,1,0:T(8,128)} %reshape.351) | data formatting | bytes 4194304
  96.5 89.5 %while.17 = (s32[]{:T(128)}, f32[8,64,128]{2,1,0:T(8,128)S(1)}, f32[8]{0:T(128)S(1)}, f32[4,256,8,64]{1,0,3,2:T(4,128)}, f32[4,256,8]{1,2,0:T(8,128)S(1)}, /*ind...) while((s32[]{:T(128)}, f32[8,64,128]{2,1,0:T(8,128)S(1)}, ...), condition=%wide.region_3.4_spmd.clone, body=%wide.region_0.3_spmd.clone.sunk | while | flops 909056064 | bytes 7901610 | solution.py:141
  98.7 3.5 %fusion.182 = f32[256,8,64]{0,2,1:T(8,128)S(1)} fusion(f32[256,256]{1,0:T(8,128)S(1)} %fusion.181, f32[8,256]{1,0:T(8,128)S(1)} %add_bitcast_fusion.4, pred[256,256]{1,0:T(8,128)(4,1)S(1)} %iota_compare_fusion.2, f32[4,256,8,64]{1,3,2,0:T(8,128)} %get-tuple-element.315, s32[]{:T(128)} %get-tuple-element.296, f32[256,8]{0,1:T(8,128)S(1)} %dynamic-slice_bitcast_fusion.7), kind=kOutput, calls=%fused_computation.5.clone.1 | convolution fusion | flops 404357120 | bytes 1401344 | tf_op jit(solution)/shard_map/while/body/eval_jaxpr/hts,shp->thp/dot_general | solution.py:62
  104.8 12.3 %dynamic_update_slice.14 = f32[4,256,8,64]{1,0,3,2:T(4,128)} dynamic-update-slice(f32[4,256,8,64]{1,0,3,2:T(4,128)} %get-tuple-element.299, f32[1,256,8,64]{1,0,3,2:T(1,128)S(1)} %copy.63, s32[]{:T(128)} %get-tuple-element.296, s32[]{:T(128)} %constant.25.clone.1..sunk, s32[]{:T(128)} %constant.25.clone.1..sunk, s32[]{:T(128)} %constant.25.clone.1..sunk) | dynamic-update-slice | bytes 1048580 | tf_op jit(solution)/shard_map/while/body/jit(dynamic_update_index_in_dim)/dynamic_update_slice | solution.py:141
  127.1 12.3 %dynamic_update_slice.14 = f32[4,256,8,64]{1,0,3,2:T(4,128)} dynamic-update-slice(f32[4,256,8,64]{1,0,3,2:T(4,128)} %get-tuple-element.299, f32[1,256,8,64]{1,0,3,2:T(1,128)S(1)} %copy.63, s32[]{:T(128)} %get-tuple-element.296, s32[]{:T(128)} %constant.25.clone.1..sunk, s32[]{:T(128)} %constant.25.clone.1..sunk, s32[]{:T(128)} %constant.25.clone.1..sunk) | dynamic-update-slice | bytes 1048580 | tf_op jit(solution)/shard_map/while/body/jit(dynamic_update_index_in_dim)/dynamic_update_slice | solution.py:141
  149.5 12.3 %dynamic_update_slice.14 = f32[4,256,8,64]{1,0,3,2:T(4,128)} dynamic-update-slice(f32[4,256,8,64]{1,0,3,2:T(4,128)} %get-tuple-element.299, f32[1,256,8,64]{1,0,3,2:T(1,128)S(1)} %copy.63, s32[]{:T(128)} %get-tuple-element.296, s32[]{:T(128)} %constant.25.clone.1..sunk, s32[]{:T(128)} %constant.25.clone.1..sunk, s32[]{:T(128)} %constant.25.clone.1..sunk) | dynamic-update-slice | bytes 1048580 | tf_op jit(solution)/shard_map/while/body/jit(dynamic_update_index_in_dim)/dynamic_update_slice | solution.py:141
  171.9 12.3 %dynamic_update_slice.14 = f32[4,256,8,64]{1,0,3,2:T(4,128)} dynamic-update-slice(f32[4,256,8,64]{1,0,3,2:T(4,128)} %get-tuple-element.299, f32[1,256,8,64]{1,0,3,2:T(1,128)S(1)} %copy.63, s32[]{:T(128)} %get-tuple-element.296, s32[]{:T(128)} %constant.25.clone.1..sunk, s32[]{:T(128)} %constant.25.clone.1..sunk, s32[]{:T(128)} %constant.25.clone.1..sunk) | dynamic-update-slice | bytes 1048580 | tf_op jit(solution)/shard_map/while/body/jit(dynamic_update_index_in_dim)/dynamic_update_slice | solution.py:141
  188.5 17.1 %all-reduce = f32[64]{0:T(128)S(1)} all-reduce(f32[64]{0:T(128)S(1)} %dynamic-update-slice), channel_id=2, replica_groups=mesh['seq_0'=4,'seq_1'=8,'head'=8] {'seq_1'}, use_global_device_ids=true, to_apply=%add | all-reduce | flops 64 | bytes 512
  205.7 21.2 %all-gather.8.cloned.1.call-done = f32[64,64,128]{2,1,0:T(8,128)} async-done(((f32[8,64,128]{2,1,0:T(8,128)}), f32[64,64,128]{2,1,0:T(8,128)}) %all-gather.8.cloned.1.call-update) | async-done | bytes 2097168 | tf_op jit(solution)/shard_map/all_gather | solution.py:32
  229.4 7.8 %all-gather.2 = f32[4,1,8]{2,1,0:T(1,128)S(1)} all-gather(f32[1,1,8]{2,1,0:T(1,128)S(1)} %get-tuple-element.197), channel_id=1, replica_groups=mesh['seq_0'=4,'seq_1'=8,'head'=8] {'seq_0'}, dimensions={0}, use_global_device_ids=true | all-gather | bytes 160 | tf_op jit(solution)/shard_map/all_gather | solution.py:32
  240.7 12.9 %all-gather.6.cloned.1.call-done = f32[4,8,64,128]{3,2,1,0:T(8,128)} async-done(((f32[1,8,64,128]{3,2,1,0:T(8,128)}), f32[4,8,64,128]{3,2,1,0:T(8,128)}) %all-gather.6.cloned.1.call-update) | async-done | bytes 1048592 | tf_op jit(solution)/shard_map/all_gather | solution.py:32
  253.7 6.1 %multiply_add_fusion = f32[1024,8,64]{0,2,1:T(8,128)} fusion(f32[1024,8,64]{0,2,1:T(8,128)} %reshape.241, f32[1024,8]{0,1:T(8,128)S(1)} %bitcast.189, f32[1024,256]{1,0:T(8,128)S(1)} %bitcast.186, f32[4,8,64,128]{3,2,1,0:T(8,128)} %all-gather.6.cloned.1.call-done, f32[64,64,128]{2,1,0:T(8,128)} %all-gather.8.cloned.1.call-done, ...), kind=kOutput, calls=%fused_computation.64 | convolution fusion | flops 808714240 | bytes 7903756 | tf_op jit(solution)/shard_map/tn,hpn->thp/dot_general | solution.py:160
  262.7 7.4 %multiply_reduce_fusion = (f32[1024]{0:T(1024)S(1)}, f32[1024,512]{1,0:T(8,128)}) fusion(f32[1024,512]{1,0:T(8,128)} %copy.52, bf16[1024,2048]{1,0:T(8,128)(2,1)} %bitcast, bf16[2048,512]{1,0:T(8,128)(2,1)} %param.16), kind=kOutput, calls=%fused_computation.62 | convolution fusion | flops 2151152640 | bytes 10489856 | tf_op jit(solution)/shard_map/dot_general | solution.py:106
  270.1 9.5 %all_to_all.11 = f32[8,1,1024]{2,1,0:T(1,128)S(1)} all-to-all(f32[8,1,1024]{2,1,0:T(1,128)S(1)} %broadcast_in_dim.43), channel_id=1, replica_groups=mesh['seq_0'=4,'seq_1'=8,'head'=8] {'head'}, dimensions={0} | all-to-all | bytes 65536 | tf_op jit(solution)/shard_map/all_to_all | solution.py:44
  279.6 6.9 %convolution_convert_fusion = bf16[1024,2048]{1,0:T(8,128)(2,1)} fusion(bf16[512,2048]{1,0:T(8,128)(2,1)S(1)} %copy-done, f32[512]{0:T(512)S(1)} %copy-done.10, f32[1024]{0:T(1024)S(1)} %add_rsqrt_fusion, f32[1024,512]{1,0:T(8,128)} %copy.52, f32[1024,512]{1,0:T(8,128)} %get-tuple-element.209), kind=kOutput, calls=%fused_computation.49 | convolution fusion | flops 2153775104 | bytes 10491904 | tf_op jit(solution)/shard_map/dot_general | solution.py:168
  286.6 40.4 %reduce-scatter.2.cloned.1.call-done = bf16[128,2048]{1,0:T(8,128)(2,1)} async-done(((bf16[1024,2048]{1,0:T(8,128)(2,1)}), bf16[128,2048]{1,0:T(8,128)(2,1)}) %reduce-scatter.2.cloned.1.call-update) | async-done | bytes 524304 | tf_op jit(solution)/shard_map/reduce_scatter | solution.py:167
  (131 shorter events, 54.8 us)
Async XLA Ops:
  6.5 273.1 %copy-start = (bf16[512,2048]{1,0:T(8,128)(2,1)S(1)}, bf16[512,2048]{1,0:T(8,128)(2,1)}, u32[]{:S(2)}) copy-start(bf16[512,2048]{1,0:T(8,128)(2,1)} %param.25) | copy-start | bytes 6291460
  10.2 4.8 %copy-start.6 = (f32[4,256]{1,0:T(4,128)S(1)}, f32[4,256]{1,0:T(4,128)}, u32[]{:S(2)}) copy-start(f32[4,256]{1,0:T(4,128)} %param.20) | copy-start | bytes 12292
  10.2 4.8 %copy-start.5 = (f32[4,512]{1,0:T(4,128)S(1)}, f32[4,512]{1,0:T(4,128)}, u32[]{:S(2)}) copy-start(f32[4,512]{1,0:T(4,128)} %param.19) | copy-start | bytes 24580
  10.2 54.3 %all-to-all-start = ((bf16[8,128,2048]{2,1,0:T(8,128)(2,1)}), bf16[8,128,2048]{2,1,0:T(8,128)(2,1)}, u32[]{:S(2)}, u32[]{:S(2)}) async-start(bf16[8,128,2048]{2,1,0:T(8,128)(2,1)} %stack.2), calls=%async_computation | async-start | bytes 8388608 | tf_op jit(solution)/shard_map/all_to_all | solution.py:101
  14.9 212.0 %all-gather.8.cloned.1.call-start = ((), (), s32[]{:S(2)}) async-start(), calls=%async_computation.5 | async-start | bytes 2359296 | tf_op jit(solution)/shard_map/all_gather | solution.py:32
  64.6 7.9 %copy-start.9 = (bf16[2048,512]{1,0:T(8,128)(2,1)S(1)}, bf16[2048,512]{1,0:T(8,128)(2,1)}, u32[]{:S(2)}) copy-start(bf16[2048,512]{1,0:T(8,128)(2,1)} %param.15) | copy-start | bytes 6291460
  68.5 12.4 %copy-start.3 = (bf16[2048,8]{0,1:T(8,128)(2,1)S(1)}, bf16[2048,8]{0,1:T(8,128)(2,1)}, u32[]{:S(2)}) copy-start(bf16[2048,8]{0,1:T(8,128)(2,1)} %param.18) | copy-start | bytes 98308
  68.5 12.4 %copy-start.7 = (f32[8]{0:T(128)S(1)}, f32[8]{0:T(128)}, u32[]{:S(2)}) copy-start(f32[8]{0:T(128)} %param.22) | copy-start | bytes 100
  68.5 12.4 %copy-start.8 = (f32[8]{0:T(128)S(1)}, f32[8]{0:T(128)}, u32[]{:S(2)}) copy-start(f32[8]{0:T(128)} %param.21) | copy-start | bytes 100
  68.5 15.8 %collective-permute-start.1 = (f32[3,256]{1,0:T(4,128)S(1)}, f32[3,256]{1,0:T(4,128)S(1)}, u32[]{:S(2)}, u32[]{:S(2)}) collective-permute-start(f32[3,256]{1,0:T(4,128)S(1)} %slice.215), channel_id=1, source_target_pairs={{0,8},{8,16},{16,24},{24,32},{32,40},{40,48},{48,56},{56,64},{64,7... | collective-permute-start | bytes 9224 | tf_op jit(solution)/shard_map/ppermute | solution.py:18
  77.0 9.0 %collective-permute-start = (f32[3,512]{1,0:T(4,128)S(1)}, f32[3,512]{1,0:T(4,128)S(1)}, u32[]{:S(2)}, u32[]{:S(2)}) collective-permute-start(f32[3,512]{1,0:T(4,128)S(1)} %slice.210), channel_id=1, source_target_pairs={{0,8},{8,16},{16,24},{24,32},{32,40},{40,48},{48,56},{56,64},{64,7... | collective-permute-start | bytes 18440 | tf_op jit(solution)/shard_map/ppermute | solution.py:18
  92.7 3.8 %copy-start.4 = (f32[8]{0:T(128)S(1)}, f32[8]{0:T(128)}, u32[]{:S(2)}) copy-start(f32[8]{0:T(128)} %param.23) | copy-start | bytes 100
  96.5 90.5 %copy-start.11 = (u32[256]{0:T(256)S(1)}, u32[256]{0:T(256)}, u32[]{:S(2)}) copy-start(u32[256]{0:T(256)} %constant.70) | copy-start | bytes 3076
  186.0 0.7 copy-start.1
  186.7 67.0 %all-gather.6.cloned.1.call-start = ((), (), s32[]{:S(2)}) async-start(), calls=%async_computation.3 | async-start | bytes 1310720 | tf_op jit(solution)/shard_map/all_gather | solution.py:32
  229.4 97.6 %reduce-scatter.2.cloned.1.call-start = ((), (), s32[]{:S(2)}) async-start(), calls=%async_computation.4 | async-start | bytes 4718592 | tf_op jit(solution)/shard_map/reduce_scatter | solution.py:167
  237.3 16.4 %copy-start.2 = (f32[4,256,256]{2,1,0:T(8,128)S(1)}, f32[4,256,256]{2,1,0:T(8,128)}, u32[]{:S(2)}) copy-start(f32[4,256,256]{2,1,0:T(8,128)} %get-tuple-element.329) | copy-start | bytes 3145732
  262.7 17.0 %copy-start.10 = (f32[512]{0:T(512)S(1)}, f32[512]{0:T(512)}, u32[]{:S(2)}) copy-start(f32[512]{0:T(512)} %param.24) | copy-start | bytes 6148
Sparse Core Ops, SparseCore 0:
  186.8 40.0 all-gather.7
  229.5 24.1 all-gather.5
  286.7 40.2 reduce-scatter.1
